TPU v7x, 32 devices: a whole 2x2x4 slice. The times are simulated.
32 devices in a mesh: rows: 8 (over z, y), mem: 4 (over x, core).
Axes of the slice: x: 2, y: 2, z: 4, core: 2. Of those that a mesh axis runs over, the one named last changes fastest.
Arguments:
- control: bfloat16 [16, 32, 2, 512, 512], P('mem', None, None, 'rows'), may hold values from -6 to 6
- vert_root: float32 [32, 32], replicated, may hold values from -1 to 1
- loc_spec: float32 [512], replicated, may hold values from 0.1 to 1
- legendre: bfloat16 [512, 512, 768], P('rows'), as said below
- wave_table: int32 [512], replicated, may hold values from 0 to 511, as said below
- lat_order: int32 [768], replicated, may hold values from 0 to 767, each once
- perturb: bfloat16 [768, 16, 32, 1536], P('rows', None, 'mem'), may hold values from -3 to 3
Outputs:
- increment: bfloat16 [768, 32, 1536], P('rows', 'mem')
Inputs may be any that keep to these rules, and one draw needn't show every extreme that they name: `wave_table`: every zonal wavenumber 0 to 511 sits in exactly one slot; the slots held by one index of rows are pairs m and 511 - m. legendre[s, n, t] is zero where n < wave_table[s]. `lat_order`: a permutation.
All inputs are finite; a program needn't handle non-finite values.
Results may differ from a plain program's by a relative error of at most 0.0085.
Values may be sent and summed in bfloat16 or wider, within the bound.
A program may use at most 256 MiB of HBM per device.

v0:
```python
import math

import jax
import jax.numpy as jnp
from jax import lax
from jax.sharding import PartitionSpec as P

BATCHES = 2


def make_basis(wave_table, lon_count):
    longitude = lax.iota(jnp.int32, lon_count)
    phases = wave_table[:, None] * longitude[None, :] % lon_count
    angles = phases.astype(jnp.float32) * (2.0 * math.pi / lon_count)
    weights = jnp.where(wave_table == 0, 1.0, 2.0).astype(jnp.float32)[:, None]
    return jnp.stack([weights * jnp.cos(angles), -weights * jnp.sin(angles)]).astype(jnp.bfloat16)


def synthesize(level_block, legendre, lat_order, zonal_basis):
    fourier = jnp.einsum(
        "snt,klrsn->strkl", legendre, level_block, preferred_element_type=jnp.float32
    )
    fourier = jnp.take(fourier, lat_order, axis=1)
    four_shape = fourier.shape
    fourier = fourier.reshape(four_shape[0], four_shape[1], -1).astype(jnp.bfloat16)
    fourier = lax.all_to_all(fourier, "rows", split_axis=1, concat_axis=0, tiled=True)
    fourier = fourier.reshape(
        fourier.shape[0], fourier.shape[1], four_shape[2], four_shape[3], four_shape[4]
    )
    fields = jnp.einsum("sjrkl,rsx->jklx", fourier, zonal_basis, preferred_element_type=jnp.float32)
    return fields.astype(jnp.bfloat16)


def member_sum(fields, member_ptb):
    return jnp.sum(fields.astype(jnp.float32) * member_ptb.astype(jnp.float32), axis=1)


def shards(control, vert_root, loc_spec, legendre, wave_table, lat_order, perturb):
    mem_count = lax.axis_size("mem")
    members_dev, levels, _, slot_count, wave_count = control.shape
    level_share = levels // mem_count
    batch_count = BATCHES
    level_batch = level_share // batch_count
    scaled = control.astype(jnp.float32) * loc_spec
    spectra = jnp.einsum(
        "lv,kvrsn->klrsn", vert_root, scaled, precision=lax.Precision.HIGHEST
    ).astype(jnp.bfloat16)
    zonal_basis = make_basis(wave_table, perturb.shape[3])
    pieces = []
    spectra = lax.all_to_all(spectra, "mem", split_axis=1, concat_axis=0, tiled=True)
    for which_batch in range(batch_count):
        first = which_batch * level_batch
        level_block = spectra[:, first : first + level_batch]
        fields = synthesize(level_block, legendre, lat_order, zonal_basis)
        pieces.append(member_sum(fields, perturb[:, :, first : first + level_batch]))
    return jnp.concatenate(pieces, axis=1).astype(jnp.bfloat16)


def solution(mesh):
    return jax.shard_map(
        shards,
        mesh=mesh,
        in_specs=(
            P("mem", None, None, "rows", None),
            P(),
            P(),
            P("rows", None, None),
            P(),
            P(),
            P("rows", None, "mem", None),
        ),
        out_specs=P("rows", "mem", None),
        check_vma=False,
    )
```

profile of v0, /device:TPU:0, one launch (start us, length us, event | category | flops | bytes accessed | tf_op | source)
XLA Modules:
  0.0 1313.2 jit_solution(8181437447585551071)
XLA Ops:
  0.0 0.0 copy-start
  0.0 19.2 %convert_multiply_fusion = f32[4,32,2,64,512]{4,3,2,1,0:T(8,128)} fusion(bf16[4,32,2,64,512]{4,3,2,1,0:T(8,128)(2,1)} %param.9, f32[512]{0:T(512)} %param.11), kind=kLoop, calls=%fused_computation.12 | loop fusion | flops 16777216 | bytes 50333696 | tf_op jit(solution)/shard_map/mul | solution.py:44
  19.2 0.0 copy-done
  19.2 59.0 %convert_bitcast_fusion = bf16[4,32,2,64,512]{4,1,3,2,0:T(8,128)(2,1)} fusion(f32[4,32,2,64,512]{4,3,2,1,0:T(8,128)} %convert_multiply_fusion, f32[32,32]{1,0:T(8,128)S(1)} %copy-done), kind=kOutput, calls=%fused_computation.16 | convolution fusion | flops 3229614080 | bytes 50335744 | tf_op jit(solution)/shard_map/lv,kvrsn->klrsn/dot_general | solution.py:45
  78.2 16.8 %copy.73 = bf16[4,32,2,64,512]{4,3,2,0,1:T(8,128)(2,1)} copy(bf16[4,32,2,64,512]{4,1,3,2,0:T(8,128)(2,1)} %convert_bitcast_fusion) | data formatting | bytes 33554432 | tf_op jit(solution)/shard_map/convert_element_type | solution.py:47
  95.0 0.0 copy-start.2
  95.0 7.1 all-to-all-start
  102.1 0.0 copy-done.2
  102.2 0.6 compare_and_fusion
  102.7 183.1 %all-to-all-done = bf16[4,32,2,64,512]{4,3,2,0,1:T(8,128)(2,1)} async-done(((bf16[4,32,2,64,512]{4,3,2,0,1:T(8,128)(2,1)}), bf16[4,32,2,64,512]{4,3,2,0,1:T(8,128)(2,1)}, u32[]{:S(2)}, u32[]{:S(2)}) %all-to-all-start) | async-done | bytes 16777248 | tf_op jit(solution)/shard_map/all_to_all | solution.py:50
  285.8 22.2 %copy.107 = bf16[4,4,8,2,64,512]{5,0,1,3,2,4:T(4,128)(2,1)} copy(bf16[4,4,8,2,64,512]{5,4,3,0,2,1:T(8,128)(2,1)} %bitcast.3) | data formatting | bytes 33554432 | tf_op jit(solution)/shard_map/all_to_all | solution.py:50
  308.0 23.7 %all_to_all.38 = bf16[16,8,2,64,512]{4,0,2,1,3:T(8,128)(2,1)} reshape(bf16[4,4,8,2,64,512]{5,1,0,3,2,4:T(4,128)(2,1)} %bitcast.64) | data formatting | bytes 33554432 | tf_op jit(solution)/shard_map/all_to_all | solution.py:50
  331.8 25.4 %fusion.11 = bf16[64,768,2,16,4]{1,3,2,4,0:T(8,128)(2,1)} fusion(bf16[16,8,2,64,512]{4,0,2,1,3:T(8,128)(2,1)} %all_to_all.38, bf16[64,512,768]{2,1,0:T(8,128)(2,1)} %param.12), kind=kOutput, calls=%fused_computation.18 | convolution fusion | flops 6442450944 | bytes 79691776 | tf_op jit(solution)/shard_map/snt,klrsn->strkl/dot_general | solution.py:20
  357.2 25.6 %fusion.8 = bf16[64,768,2,16,4]{1,3,2,4,0:T(8,128)(2,1)} fusion(bf16[16,8,2,64,512]{4,0,2,1,3:T(8,128)(2,1)} %all_to_all.38, bf16[64,512,768]{2,1,0:T(8,128)(2,1)} %param.12), kind=kOutput, calls=%fused_computation.17 | convolution fusion | flops 6442450944 | bytes 79691776 | tf_op jit(solution)/shard_map/snt,klrsn->strkl/dot_general | solution.py:20
  382.8 42.8 %copy.75 = bf16[64,768,2,16,4]{0,3,2,4,1:T(8,128)(2,1)} copy(bf16[64,768,2,16,4]{1,3,2,4,0:T(8,128)(2,1)} %fusion.8) | data formatting | bytes 25165824 | tf_op jit(solution)/shard_map/snt,klrsn->strkl/transpose | solution.py:20
  425.5 27.4 %gather_fusion = bf16[768,64,2,16,4]{1,3,2,4,0:T(8,128)(2,1)} fusion(bf16[64,768,2,16,4]{0,3,2,4,1:T(8,128)(2,1)} %copy.75, s32[1024]{0:T(1024)S(1)} %pad_clamp_fusion), kind=kCustom, calls=%fused_computation.clone | custom fusion | bytes 25168896 | tf_op jit(solution)/shard_map/jit(_take)/gather | solution.py:23
  452.9 36.6 %copy.76 = bf16[768,64,2,16,4]{0,3,4,2,1:T(8,128)(2,1)} copy(bf16[768,64,2,16,4]{1,3,2,4,0:T(8,128)(2,1)} %gather_fusion) | data formatting | bytes 25165824 | tf_op jit(solution)/shard_map/jit(_take)/gather | solution.py:23
  489.5 43.0 %copy.83 = bf16[64,768,2,16,4]{0,3,2,4,1:T(8,128)(2,1)} copy(bf16[64,768,2,16,4]{1,3,2,4,0:T(8,128)(2,1)} %fusion.11) | data formatting | bytes 25165824 | tf_op jit(solution)/shard_map/snt,klrsn->strkl/transpose | solution.py:20
  532.4 27.4 %gather_fusion.1 = bf16[768,64,2,16,4]{1,3,2,4,0:T(8,128)(2,1)} fusion(bf16[64,768,2,16,4]{0,3,2,4,1:T(8,128)(2,1)} %copy.83, s32[1024]{0:T(1024)S(1)} %pad_clamp_fusion), kind=kCustom, calls=%fused_computation.1.clone | custom fusion | bytes 25168896 | tf_op jit(solution)/shard_map/jit(_take)/gather | solution.py:23
  559.8 0.0 copy-start.4
  559.8 36.6 %copy.84 = bf16[768,64,2,16,4]{0,3,4,2,1:T(8,128)(2,1)} copy(bf16[768,64,2,16,4]{1,3,2,4,0:T(8,128)(2,1)} %gather_fusion.1) | data formatting | bytes 25165824 | tf_op jit(solution)/shard_map/jit(_take)/gather | solution.py:23
  596.4 0.0 copy-done.4
  596.4 16.9 %bitcast_convert_fusion.3 = (bf16[64,768,2,16,4]{1,3,4,2,0:T(8,128)(2,1)S(1)}, bf16[64,768,2,16,4]{1,3,4,2,0:T(8,128)(2,1)}) fusion(bf16[768,64,2,16,4]{0,3,4,2,1:T(8,128)(2,1)} %copy.76, pred[768]{0:T(1024)(128)(4,1)S(1)} %copy-done.4, bf16[768,64,2,16,4]{0,3,4,2,1:T(8,128)(2,1)} %copy.84), kind=kLoop, calls=%fused_computation.14 | loop fusion | flops 12582912 | bytes 50332416 | tf_op jit(solution)/shard_map/convert_element_type | solution.py:25
  613.3 9.1 copy.77
  622.4 18.0 %copy.78 = bf16[64,768,128]{2,0,1:T(8,128)(2,1)} copy(bf16[64,768,128]{1,0,2:T(8,128)(2,1)} %bitcast.65) | data formatting | bytes 25165824 | tf_op jit(solution)/shard_map/convert_element_type | solution.py:25
  640.4 6.7 all-to-all-start.1
  647.1 14.2 %copy.85 = bf16[64,768,2,16,4]{1,0,4,3,2:T(8,128)(2,1)} copy(bf16[64,768,2,16,4]{1,3,4,2,0:T(8,128)(2,1)} %get-tuple-element.13) | data formatting | bytes 25165824 | tf_op jit(solution)/shard_map/convert_element_type | solution.py:25
  661.3 18.0 %copy.86 = bf16[64,768,128]{2,0,1:T(8,128)(2,1)} copy(bf16[64,768,128]{1,0,2:T(8,128)(2,1)} %bitcast.66) | data formatting | bytes 25165824 | tf_op jit(solution)/shard_map/convert_element_type | solution.py:25
  679.3 0.0 copy-start.3
  679.3 240.5 %all-to-all-done.1 = bf16[64,768,128]{2,0,1:T(8,128)(2,1)} async-done(((bf16[64,768,128]{2,0,1:T(8,128)(2,1)}), bf16[64,768,128]{2,0,1:T(8,128)(2,1)}, u32[]{:S(2)}, u32[]{:S(2)}) %all-to-all-start.1) | async-done | bytes 12582944 | tf_op jit(solution)/shard_map/all_to_all | solution.py:26
  919.9 5.6 all-to-all-start.2
  925.5 0.0 copy-done.3
  925.5 13.8 %multiply_convert_fusion.1 = (bf16[1,512,1536]{2,1,0:T(8,128)(2,1)S(1)}, bf16[1,512,1536]{2,1,0:T(8,128)(2,1)S(1)}) fusion(s32[512]{0:T(512)S(1)} %copy-done.3, f32[512]{0:T(512)S(1)} %get-tuple-element.10, f32[512]{0:T(512)S(1)} %get-tuple-element.11), kind=kLoop, calls=%fused_computation.24 | loop fusion | flops 10223616 | bytes 3151872 | tf_op jit(solution)/shard_map/convert.2
  939.3 38.1 %fusion.23 = (bf16[96,16,4,1536]{3,2,1,0:T(4,128)(2,1)}, bf16[96,16,4,1536]{3,2,1,0:T(4,128)(2,1)}) fusion(bf16[96,16,8,1536]{3,2,1,0:T(8,128)(2,1)} %param.15), kind=kLoop, calls=%fused_computation.38 | loop fusion | bytes 75497472 | tf_op jit(solution)/shard_map/slice | solution.py:55
  977.4 24.1 %copy.80 = bf16[8,64,96,128]{2,1,0,3:T(8,128)(2,1)} copy(bf16[8,64,96,128]{3,1,2,0:T(8,128)(2,1)} %bitcast.12) | data formatting | bytes 25165824 | tf_op jit(solution)/shard_map/all_to_all | solution.py:26
  1001.5 26.2 %copy.81 = bf16[512,96,2,16,4]{0,3,2,4,1:T(8,128)(2,1)} copy(bf16[512,96,2,16,4]{1,0,4,3,2:T(8,128)(2,1)} %bitcast.62) | data formatting | bytes 25165824 | tf_op jit(solution)/shard_map/reshape | solution.py:27
  1027.7 169.6 %all-to-all-done.2 = bf16[64,768,128]{2,0,1:T(8,128)(2,1)} async-done(((bf16[64,768,128]{2,0,1:T(8,128)(2,1)}), bf16[64,768,128]{2,0,1:T(8,128)(2,1)}, u32[]{:S(2)}, u32[]{:S(2)}) %all-to-all-start.2) | async-done | bytes 12582944 | tf_op jit(solution)/shard_map/all_to_all | solution.py:26
  1197.3 24.1 %copy.88 = bf16[8,64,96,128]{2,1,0,3:T(8,128)(2,1)} copy(bf16[8,64,96,128]{3,1,2,0:T(8,128)(2,1)} %bitcast.24) | data formatting | bytes 25165824 | tf_op jit(solution)/shard_map/all_to_all | solution.py:26
  1221.4 26.2 %copy.89 = bf16[512,96,2,16,4]{0,3,2,4,1:T(8,128)(2,1)} copy(bf16[512,96,2,16,4]{1,0,4,3,2:T(8,128)(2,1)} %bitcast.63) | data formatting | bytes 25165824 | tf_op jit(solution)/shard_map/reshape | solution.py:27
  1247.6 30.4 %multiply_reduce_fusion = bf16[96,4,1536]{2,1,0:T(4,128)(2,1)} fusion(bf16[96,16,4,1536]{3,2,1,0:T(4,128)(2,1)} %get-tuple-element.7, bf16[512,96,2,16,4]{0,3,2,4,1:T(8,128)(2,1)} %copy.89, bf16[1,512,1536]{2,1,0:T(8,128)(2,1)S(1)} %get-tuple-element.9, bf16[1,512,1536]{2,1,0:T(8,128)(2,1)S(1)} %get-tuple-element.8), kind=kOutput, calls=%fused_computation.8 | convolution fusion | flops 19375521792 | bytes 35782656 | tf_op jit(solution)/shard_map/sjrkl,rsx->jklx/dot_general | solution.py:30
  1278.0 0.0 copy-start.1
  1278.0 30.6 %multiply_reduce_fusion.1 = bf16[96,4,1536]{2,1,0:T(4,128)(2,1)} fusion(bf16[96,16,4,1536]{3,2,1,0:T(4,128)(2,1)} %get-tuple-element.6, bf16[512,96,2,16,4]{0,3,2,4,1:T(8,128)(2,1)} %copy.81, bf16[1,512,1536]{2,1,0:T(8,128)(2,1)S(1)} %get-tuple-element.9, bf16[1,512,1536]{2,1,0:T(8,128)(2,1)S(1)} %get-tuple-element.8), kind=kOutput, calls=%fused_computation.9 | convolution fusion | flops 19375521792 | bytes 35782656 | tf_op jit(solution)/shard_map/sjrkl,rsx->jklx/dot_general | solution.py:30
  1308.6 4.2 pad_maximum_fusion
  1312.8 0.0 copy-done.1
  (3 shorter events, 0.0 us)
Async XLA Ops:
  0.0 19.2 %copy-start = (f32[32,32]{1,0:T(8,128)S(1)}, f32[32,32]{1,0:T(8,128)}, u32[]{:S(2)}) copy-start(f32[32,32]{1,0:T(8,128)} %param.10) | copy-start | bytes 12292
  95.0 7.1 copy-start.2
  95.0 190.8 %all-to-all-start = ((bf16[4,32,2,64,512]{4,3,2,0,1:T(8,128)(2,1)}), bf16[4,32,2,64,512]{4,3,2,0,1:T(8,128)(2,1)}, u32[]{:S(2)}, u32[]{:S(2)}) async-start(bf16[4,32,2,64,512]{4,3,2,0,1:T(8,128)(2,1)} %copy.73), calls=%async_computation | async-start | bytes 33554432 | tf_op jit(solution)/shard_map/all_to_all | solution.py:50
  559.8 36.6 %copy-start.4 = (pred[768]{0:T(1024)(128)(4,1)S(1)}, pred[768]{0:T(1024)(128)(4,1)}, u32[]{:S(2)}) copy-start(pred[768]{0:T(1024)(128)(4,1)} %compare_and_fusion) | copy-start | bytes 2308
  640.4 279.4 %all-to-all-start.1 = ((bf16[64,768,128]{2,0,1:T(8,128)(2,1)}), bf16[64,768,128]{2,0,1:T(8,128)(2,1)}, u32[]{:S(2)}, u32[]{:S(2)}) async-start(bf16[64,768,128]{2,0,1:T(8,128)(2,1)} %copy.78), calls=%async_computation.1 | async-start | bytes 25165824 | tf_op jit(solution)/shard_map/all_to_all | solution.py:26
  679.3 246.1 %copy-start.3 = (s32[512]{0:T(512)S(1)}, s32[512]{0:T(512)}, u32[]{:S(2)}) copy-start(s32[512]{0:T(512)} %param.13) | copy-start | bytes 6148
  919.9 277.4 %all-to-all-start.2 = ((bf16[64,768,128]{2,0,1:T(8,128)(2,1)}), bf16[64,768,128]{2,0,1:T(8,128)(2,1)}, u32[]{:S(2)}, u32[]{:S(2)}) async-start(bf16[64,768,128]{2,0,1:T(8,128)(2,1)} %copy.86), calls=%async_computation.2 | async-start | bytes 25165824 | tf_op jit(solution)/shard_map/all_to_all | solution.py:26
  1278.0 34.8 %copy-start.1 = (f32[32,32]{1,0:T(8,128)S(1)}, f32[32,32]{1,0:T(8,128)}, u32[]{:S(2)}) copy-start(f32[32,32]{1,0:T(8,128)} %param.10) | copy-start | bytes 12292
where the time goes:
time: 1330 us; the launch traced here: 1310 us
  waiting for transfers between devices  593 us (45%)
  local copies, waits for them, and re-layouts  474 us (36%)
  matrix products  171 us (13%)
  other arithmetic  54.7 us (4%)
  starting transfers between devices  19.4 us (1%)
    all_to_all x2, waiting for transfers between devices, synthesize(): lax.all_to_all(fourier, 'rows', split_axis=1, concat_axis=0, tiled=True)  410 us
    all_to_all x1, waiting for transfers between devices, shards(): lax.all_to_all(spectra, 'mem', split_axis=1, concat_axis=0, tiled=True)  183 us
    gather x4, local copies, waits for them, and re-layouts, synthesize(): fourier = jnp.take(fourier, lat_order, axis=1)  128 us
    transpose x2, local copies, waits for them, and re-layouts, synthesize(): jnp.einsum('snt,klrsn->strkl', legendre, level_block, preferred_element_t...  85.7 us
    dot_general x2, matrix products, synthesize(): jnp.einsum('sjrkl,rsx->jklx', fourier, zonal_basis, preferred_element_typ...  61 us
    convert_element_type x4, local copies, waits for them, and re-layouts, synthesize(): fourier.reshape(four_shape[0], four_shape[1], -1).astype(jnp.bfloat16)  59.4 us
    dot_general x1, matrix products, shards(): jnp.einsum('lv,kvrsn->klrsn', vert_root, scaled, precision=lax.Precision....  59 us
    reshape x2, local copies, waits for them, and re-layouts, synthesize(): fourier.reshape(fourier.shape[0], fourier.shape[1], four_shape[2], four_s...  52.4 us
  transfers between devices with their start and end apart: 3, of which 3 were waited for; matrix products, arithmetic and copies ran while one was open for 10% of the time, Pallas kernels for 0%

commit v1 on v0

v1 whole, which is shorter than its diff:
```python
import functools
import math

import jax
import jax.numpy as jnp
from jax import lax
from jax.experimental import pallas as pl
from jax.experimental.pallas import tpu as pltpu
from jax.sharding import PartitionSpec as P

HALVES = 2
LATS = 4
VMEM_LIMIT = 56 * 1024 * 1024


def make_basis(wave_table, lon_count):
    longitude = lax.iota(jnp.int32, lon_count)
    phases = wave_table[:, None] * longitude[None, :] % lon_count
    angles = phases.astype(jnp.float32) * (2.0 * math.pi / lon_count)
    weights = jnp.where(wave_table == 0, 1.0, 2.0).astype(jnp.float32)[:, None]
    return jnp.stack([weights * jnp.cos(angles), -weights * jnp.sin(angles)]).astype(jnp.bfloat16)


def legendre_kernel(*refs):
    specs, (leg_ref, order_ref, out_ref) = refs[:-3], refs[-3:]
    members, parts, _, levels, totals = specs[0].shape
    rows = [
        s[:, r, 0].reshape(members * levels, totals) for r in range(parts) for s in specs
    ]
    spec = jnp.concatenate(rows, axis=0)
    fourier = jnp.dot(spec, leg_ref[0], preferred_element_type=jnp.float32).astype(jnp.bfloat16)
    stored = lax.dot_general(
        order_ref[...], fourier, (((1,), (1,)), ((), ())), preferred_element_type=jnp.float32
    ).astype(jnp.bfloat16)
    lats = out_ref.shape[2]
    for d in range(out_ref.shape[0]):
        out_ref[d, 0] = stored[d * lats : (d + 1) * lats]


def legendre_step(specs, legendre, order, first, row_count):
    members, parts, slots, levels, totals = specs[0].shape
    lat_count = legendre.shape[2]
    lats = lat_count // row_count
    width = len(specs) * members * parts * levels
    flops = 2 * slots * width * lat_count * (totals + lat_count)
    return pl.pallas_call(
        legendre_kernel,
        grid=(slots,),
        out_shape=jax.ShapeDtypeStruct((row_count, slots, lats, width), jnp.bfloat16),
        in_specs=[
            pl.BlockSpec((members, parts, 1, levels, totals), lambda s: (0, 0, s, 0, 0))
            for _ in specs
        ]
        + [
            pl.BlockSpec((1, totals, lat_count), lambda s: (first + s, 0, 0)),
            pl.BlockSpec((lat_count, lat_count), lambda s: (0, 0)),
        ],
        out_specs=pl.BlockSpec((row_count, 1, lats, width), lambda s: (0, s, 0, 0)),
        compiler_params=pltpu.CompilerParams(vmem_limit_bytes=VMEM_LIMIT),
        cost_estimate=pl.CostEstimate(
            flops=flops,
            bytes_accessed=2 * slots * (totals + width) * lat_count,
            transcendentals=0,
        ),
    )(*specs, legendre, order)


def zonal_kernel(chunks, half, *refs):
    fours, (basis_ref, ptb_ref, before_ref, out_ref) = refs[:chunks], refs[chunks:]
    lats, members, levels, lon_count = ptb_ref.shape
    mem_count = lax.axis_size("mem")
    me = lax.axis_index("mem")
    share = members // mem_count
    taken = share // HALVES
    width = fours[0].shape[2] // 2
    blocks = []
    for j in range(lats):
        pairs = [f[j].T for f in fours]
        blocks.append(
            jnp.concatenate([p[r * width : (r + 1) * width] for p in pairs for r in range(2)], axis=1)
        )
    lhs = jnp.concatenate(blocks, axis=0)
    piece = 512 if lon_count % 512 == 0 else lon_count
    for x in range(0, lon_count, piece):
        field = jnp.dot(lhs, basis_ref[:, x : x + piece], preferred_element_type=jnp.float32)
        field = field.astype(jnp.bfloat16).astype(jnp.float32)
        field = field.reshape(lats, mem_count, taken, levels, piece)
        total = jnp.zeros((lats, levels, piece), jnp.float32)
        if half > 0:
            total = before_ref[:, :, x : x + piece]
        for i in range(mem_count):
            source = lax.rem(me + mem_count - i, mem_count)
            begin = source * share + half * taken
            ptb = ptb_ref[:, pl.ds(begin, taken), :, x : x + piece].astype(jnp.float32)
            total += jnp.sum(field[:, i] * ptb, axis=1)
        out_ref[:, :, x : x + piece] = total.astype(out_ref.dtype)


def zonal_step(fours, basis, perturb, half, before):
    lats, members, levels, lon_count = perturb.shape
    width = fours[0].shape[2]
    depth = basis.shape[0]
    block = math.gcd(LATS, lats)
    out_type = jnp.bfloat16 if half == HALVES - 1 else jnp.float32
    row = pl.BlockSpec((block, levels, lon_count), lambda j: (j, 0, 0))
    kept = row if half > 0 else pl.BlockSpec((1, 8, 128), lambda j: (0, 0, 0))
    return pl.pallas_call(
        functools.partial(zonal_kernel, len(fours), half),
        grid=(lats // block,),
        out_shape=jax.ShapeDtypeStruct((lats, levels, lon_count), out_type),
        in_specs=[
            pl.BlockSpec((block, f.shape[1], width), lambda j: (j, 0, 0)) for f in fours
        ]
        + [
            pl.BlockSpec((depth, lon_count), lambda j: (0, 0)),
            pl.BlockSpec((block, members, levels, lon_count), lambda j: (j, 0, 0, 0)),
            kept,
        ],
        out_specs=row,
        compiler_params=pltpu.CompilerParams(vmem_limit_bytes=VMEM_LIMIT),
        cost_estimate=pl.CostEstimate(
            flops=lats * depth * width * lon_count,
            bytes_accessed=2 * perturb.size,
            transcendentals=0,
        ),
    )(*fours, basis, perturb, before)


def ordered_basis(wave_table, parts, row_count, lon_count):
    table = wave_table.reshape(row_count, -1)
    pieces, first = [], 0
    basis = make_basis(table.reshape(-1), lon_count).reshape(2, row_count, -1, lon_count)
    for slots in parts:
        pieces.append(basis[:, :, first : first + slots].reshape(-1, lon_count))
        first += slots
    return jnp.concatenate(pieces, axis=0)


def shards(control, vert_root, loc_spec, legendre, wave_table, lat_order, perturb):
    mem_count = lax.axis_size("mem")
    row_count = lax.axis_size("rows")
    members, levels, _, slot_count, totals = control.shape
    lat_count = legendre.shape[2]
    share = levels // mem_count
    me = lax.axis_index("mem")
    root = vert_root.reshape(mem_count, share, levels).astype(jnp.bfloat16)
    root = jnp.take(root, (me + lax.iota(jnp.int32, mem_count)) % mem_count, axis=0)
    order = (lat_order[:, None] == lax.iota(jnp.int32, lat_count)[None, :]).astype(jnp.bfloat16)

    taken = members // HALVES
    eighth = slot_count // 8
    splits = [(2 * eighth, 3 * eighth, 3 * eighth), (4 * eighth, 4 * eighth)]
    partial = jnp.zeros((1, 8, 128), jnp.float32)
    for half, split in enumerate(splits):
        fours, first = [], 0
        for slots in split:
            spec = jnp.einsum(
                "dlv,kvrsn->dkrsln",
                root,
                control[half * taken : (half + 1) * taken, :, :, first : first + slots],
                preferred_element_type=jnp.float32,
            )
            spec = (spec * loc_spec).astype(jnp.bfloat16)
            specs = [spec[0]] + [
                lax.ppermute(spec[i], "mem", [(d, (d + i) % mem_count) for d in range(mem_count)])
                for i in range(1, mem_count)
            ]
            four = legendre_step(specs, legendre, order, first, row_count)
            four = lax.all_to_all(four, "rows", split_axis=0, concat_axis=0, tiled=True)
            four = four.reshape(row_count * slots, four.shape[2], four.shape[3]).swapaxes(0, 1)
            fours.append(four)
            first += slots
        basis = ordered_basis(wave_table, split, row_count, perturb.shape[3])
        partial = zonal_step(fours, basis, perturb, half, partial)
    return partial


def solution(mesh):
    return jax.shard_map(
        shards,
        mesh=mesh,
        in_specs=(
            P("mem", None, None, "rows", None),
            P(),
            P(),
            P("rows", None, None),
            P(),
            P(),
            P("rows", None, "mem", None),
        ),
        out_specs=P("rows", "mem", None),
        check_vma=False,
    )
```

time: 1330 us -> 682 us (0.51)
  local copies, waits for them, and re-layouts: 474 us -> 56.4 us
  waiting for transfers between devices: 593 us -> 331 us
  Pallas kernels: 0 us -> 216 us
  matrix products: 171 us -> 17.5 us
  other arithmetic: 54.7 us -> 20.2 us
  starting transfers between devices: 19.4 us -> 35.4 us
    all_to_all x3 -> x5, waiting for transfers between devices: 593 us -> 146 us  [shards(): four = lax.all_to_all(four, 'rows', split_axis=0, concat_axis=0, tiled=True)]
    pallas_call x0 -> x7, Pallas kernels: none -> 216 us  [the longest x5 141 us: legendre_step(): pl.pallas_call(legendre_kernel, grid=(slots,), out_shape=jax.ShapeDtypeSt...]
    ppermute x0 -> x15, waiting for transfers between devices: none -> 185 us  [shards(): lax.ppermute(spec[i], 'mem', [(d, (d + i) % mem_count) for d in range(mem...]
    dot_general x5, matrix products: 171 us -> 17.5 us  [shards(): jnp.einsum('dlv,kvrsn->dkrsln', root, control[half * taken:(half + 1) * t...]
    gather x4 -> x1, local copies, waits for them, and re-layouts: 128 us -> 0.56 us  [shards(): jnp.take(root, (me + lax.iota(jnp.int32, mem_count)) % mem_count, axis=0)]
    transpose x2 -> x0, local copies, waits for them, and re-layouts: 85.7 us -> none  [synthesize(): jnp.einsum('snt,klrsn->strkl', legendre, level_block, preferred_element_t...]
    convert_element_type x5 -> x0, local copies, waits for them, and re-layouts: 76.2 us -> none  [the longest x4 59.4 us: synthesize(): fourier.reshape(four_shape[0], four_shape[1], -1).astype(jnp.bfloat16)]
    all_to_all x4 -> x5, local copies, waits for them, and re-layouts: 94.2 us -> 31.2 us  [shards(): four = lax.all_to_all(four, 'rows', split_axis=0, concat_axis=0, tiled=True)]
  transfers between devices with their start and end apart: 3 -> 20, of which waited for: 3 -> 18; matrix products, arithmetic and copies ran while one was open for 10% -> 11% of each run, Pallas kernels for 0% -> 24%
where the time goes in v1:
time: 682 us; the launch traced here: 676 us
  waiting for transfers between devices  331 us (49%)
  Pallas kernels  216 us (32%)
  local copies, waits for them, and re-layouts  56.4 us (8%)
  starting transfers between devices  35.4 us (5%)
  other arithmetic  20.2 us (3%)
  matrix products  17.5 us (3%)
    ppermute x15, waiting for transfers between devices, shards(): lax.ppermute(spec[i], 'mem', [(d, (d + i) % mem_count) for d in range(mem...  185 us
    all_to_all x5, waiting for transfers between devices, shards(): four = lax.all_to_all(four, 'rows', split_axis=0, concat_axis=0, tiled=True)  146 us
    pallas_call x5, Pallas kernels, legendre_step(): pl.pallas_call(legendre_kernel, grid=(slots,), out_shape=jax.ShapeDtypeSt...  141 us
    pallas_call x2, Pallas kernels, zonal_step(): pl.pallas_call(functools.partial(zonal_kernel, len(fours), half), grid=(l...  74.8 us
    all_to_all x5, local copies, waits for them, and re-layouts, shards(): four = lax.all_to_all(four, 'rows', split_axis=0, concat_axis=0, tiled=True)  31.2 us
    all_to_all x5, starting transfers between devices, shards(): four = lax.all_to_all(four, 'rows', split_axis=0, concat_axis=0, tiled=True)  26.4 us
    dot_general x5, matrix products, shards(): jnp.einsum('dlv,kvrsn->dkrsln', root, control[half * taken:(half + 1) * t...  17.5 us
    another operation x1, other arithmetic  13.7 us
  transfers between devices with their start and end apart: 20, of which 18 were waited for; matrix products, arithmetic and copies ran while one was open for 11% of the time, Pallas kernels for 24%

profile of v1, /device:TPU:0, one launch (start us, length us, event | category | flops | bytes accessed | tf_op | source)
XLA Modules:
  0.0 676.3 jit_solution(1094763747190144840)
XLA Ops:
  0.8 1.8 slice.102
  3.1 1.7 fusion.14
  5.8 2.4 collective-permute-start.8
  9.0 1.3 fusion.13.refs_5_
  10.3 10.1 %collective-permute-done.8.refs_3_ = bf16[2,2,16,8,512]{4,3,2,1,0:T(8,128)(2,1)S(1)} collective-permute-done((bf16[2,2,16,8,512]{4,3,2,1,0:T(8,128)(2,1)S(1)}, bf16[2,2,16,8,512]{4,3,2,1,0:T(8,128)(2,1)S(1)}, u32[]{:S(2)}, u32[]{:S(2)}) %collective-permute-start.8) | collective-permute-done | bytes 524320 | tf_op jit(solution)/shard_map/ppermute | solution.py:165
  20.4 12.2 %collective-permute-done.7.refs_2_ = bf16[2,2,16,8,512]{4,3,2,1,0:T(8,128)(2,1)S(1)} collective-permute-done((bf16[2,2,16,8,512]{4,3,2,1,0:T(8,128)(2,1)S(1)}, bf16[2,2,16,8,512]{4,3,2,1,0:T(8,128)(2,1)S(1)}, u32[]{:S(2)}, u32[]{:S(2)}) %collective-permute-start.7) | collective-permute-done | bytes 524320 | tf_op jit(solution)/shard_map/ppermute | solution.py:165
  33.5 18.3 %shard_map.75 = bf16[8,16,96,128]{3,2,1,0:T(8,128)(2,1)} custom-call(bf16[2,2,16,8,512]{4,3,2,1,0:T(8,128)(2,1)} %get-tuple-element.32.refs_0_, bf16[2,2,16,8,512]{4,3,2,1,0:T(8,128)(2,1)} %copy-done.15, bf16[2,2,16,8,512]{4,3,2,1,0:T(8,128)(2,1)} %copy-done.14, bf16[2,2,16,8,512]{4,3,2,1,0:T(8,128)(2,1)} %copy-done.13, bf16[64,512,768]{2,1,0:T(8,128)(2,1)} %refs_4_.10, ...), custom_call_target="tpu_custom_call" | custom-call | flops 4026531840 | bytes 15728640 | tf_op jit(solution)/shard_map/pallas_call | solution.py:46
  51.8 5.9 all-to-all-start.2
  57.8 5.5 fusion.28
  63.3 2.5 fusion.7
  67.0 1.4 collective-permute-start.13
  68.6 15.3 %collective-permute-done.14.refs_3_ = bf16[2,2,24,8,512]{4,3,2,1,0:T(8,128)(2,1)S(1)} collective-permute-done((bf16[2,2,24,8,512]{4,3,2,1,0:T(8,128)(2,1)S(1)}, bf16[2,2,24,8,512]{4,3,2,1,0:T(8,128)(2,1)S(1)}, u32[]{:S(2)}, u32[]{:S(2)}) %collective-permute-start.14) | collective-permute-done | bytes 786464 | tf_op jit(solution)/shard_map/ppermute | solution.py:165
  83.9 19.5 %collective-permute-done.13.refs_2_ = bf16[2,2,24,8,512]{4,3,2,1,0:T(8,128)(2,1)S(1)} collective-permute-done((bf16[2,2,24,8,512]{4,3,2,1,0:T(8,128)(2,1)S(1)}, bf16[2,2,24,8,512]{4,3,2,1,0:T(8,128)(2,1)S(1)}, u32[]{:S(2)}, u32[]{:S(2)}) %collective-permute-start.13) | collective-permute-done | bytes 786464 | tf_op jit(solution)/shard_map/ppermute | solution.py:165
  104.6 26.5 %shard_map.77 = bf16[8,24,96,128]{3,2,1,0:T(8,128)(2,1)} custom-call(bf16[2,2,24,8,512]{4,3,2,1,0:T(8,128)(2,1)} %get-tuple-element.22.refs_0_, bf16[2,2,24,8,512]{4,3,2,1,0:T(8,128)(2,1)} %copy-done.11, bf16[2,2,24,8,512]{4,3,2,1,0:T(8,128)(2,1)} %copy-done.9, bf16[2,2,24,8,512]{4,3,2,1,0:T(8,128)(2,1)} %copy-done.7, bf16[64,512,768]{2,1,0:T(8,128)(2,1)} %refs_4_.10, ...), custom_call_target="tpu_custom_call" | custom-call | flops 6039797760 | bytes 23592960 | tf_op jit(solution)/shard_map/pallas_call | solution.py:46
  131.2 6.0 all-to-all-start.4
  137.1 4.4 fusion.6
  143.5 17.1 %collective-permute-done.11.refs_3_ = bf16[2,2,24,8,512]{4,3,2,1,0:T(8,128)(2,1)S(1)} collective-permute-done((bf16[2,2,24,8,512]{4,3,2,1,0:T(8,128)(2,1)S(1)}, bf16[2,2,24,8,512]{4,3,2,1,0:T(8,128)(2,1)S(1)}, u32[]{:S(2)}, u32[]{:S(2)}) %collective-permute-start.11) | collective-permute-done | bytes 786464 | tf_op jit(solution)/shard_map/ppermute | solution.py:165
  160.6 16.9 %collective-permute-done.10.refs_2_ = bf16[2,2,24,8,512]{4,3,2,1,0:T(8,128)(2,1)S(1)} collective-permute-done((bf16[2,2,24,8,512]{4,3,2,1,0:T(8,128)(2,1)S(1)}, bf16[2,2,24,8,512]{4,3,2,1,0:T(8,128)(2,1)S(1)}, u32[]{:S(2)}, u32[]{:S(2)}) %collective-permute-start.10) | collective-permute-done | bytes 786464 | tf_op jit(solution)/shard_map/ppermute | solution.py:165
  179.4 26.5 %shard_map.76 = bf16[8,24,96,128]{3,2,1,0:T(8,128)(2,1)} custom-call(bf16[2,2,24,8,512]{4,3,2,1,0:T(8,128)(2,1)} %get-tuple-element.26.refs_0_, bf16[2,2,24,8,512]{4,3,2,1,0:T(8,128)(2,1)} %copy-done.12, bf16[2,2,24,8,512]{4,3,2,1,0:T(8,128)(2,1)} %copy-done.10, bf16[2,2,24,8,512]{4,3,2,1,0:T(8,128)(2,1)} %copy-done.8, bf16[64,512,768]{2,1,0:T(8,128)(2,1)} %refs_4_.10, ...), custom_call_target="tpu_custom_call" | custom-call | flops 6039797760 | bytes 23592960 | tf_op jit(solution)/shard_map/pallas_call | solution.py:46
  205.9 34.1 %all-to-all-done.4 = bf16[8,24,96,128]{3,2,1,0:T(8,128)(2,1)} async-done(((bf16[8,24,96,128]{3,2,1,0:T(8,128)(2,1)}), bf16[8,24,96,128]{3,2,1,0:T(8,128)(2,1)}, u32[]{:S(2)}, u32[]{:S(2)}) %all-to-all-start.4) | async-done | bytes 4718624 | tf_op jit(solution)/shard_map/all_to_all | solution.py:169
  240.0 4.8 all-to-all-start.3
  244.8 5.3 fusion.29
  250.0 3.3 fusion
  254.6 1.5 collective-permute-start.1
  256.3 20.8 %collective-permute-done.2.refs_3_ = bf16[2,2,32,8,512]{4,3,2,1,0:T(8,128)(2,1)S(1)} collective-permute-done((bf16[2,2,32,8,512]{4,3,2,1,0:T(8,128)(2,1)S(1)}, bf16[2,2,32,8,512]{4,3,2,1,0:T(8,128)(2,1)S(1)}, u32[]{:S(2)}, u32[]{:S(2)}) %collective-permute-start.2) | collective-permute-done | bytes 1048608 | tf_op jit(solution)/shard_map/ppermute | solution.py:165
  277.2 25.3 %collective-permute-done.1.refs_2_ = bf16[2,2,32,8,512]{4,3,2,1,0:T(8,128)(2,1)S(1)} collective-permute-done((bf16[2,2,32,8,512]{4,3,2,1,0:T(8,128)(2,1)S(1)}, bf16[2,2,32,8,512]{4,3,2,1,0:T(8,128)(2,1)S(1)}, u32[]{:S(2)}, u32[]{:S(2)}) %collective-permute-start.1) | collective-permute-done | bytes 1048608 | tf_op jit(solution)/shard_map/ppermute | solution.py:165
  303.9 34.8 %shard_map.73 = bf16[8,32,96,128]{3,2,1,0:T(8,128)(2,1)} custom-call(bf16[2,2,32,8,512]{4,3,2,1,0:T(8,128)(2,1)} %get-tuple-element.16.refs_0_, bf16[2,2,32,8,512]{4,3,2,1,0:T(8,128)(2,1)} %copy-done.5, bf16[2,2,32,8,512]{4,3,2,1,0:T(8,128)(2,1)} %copy-done.3, bf16[2,2,32,8,512]{4,3,2,1,0:T(8,128)(2,1)} %copy-done.1, bf16[64,512,768]{2,1,0:T(8,128)(2,1)} %refs_4_.10, ...), custom_call_target="tpu_custom_call" | custom-call | flops 8053063680 | bytes 31457280 | tf_op jit(solution)/shard_map/pallas_call | solution.py:46
  338.7 9.7 %all-to-all-done.3 = bf16[8,24,96,128]{3,2,1,0:T(8,128)(2,1)} async-done(((bf16[8,24,96,128]{3,2,1,0:T(8,128)(2,1)}), bf16[8,24,96,128]{3,2,1,0:T(8,128)(2,1)}, u32[]{:S(2)}, u32[]{:S(2)}) %all-to-all-start.3) | async-done | bytes 4718624 | tf_op jit(solution)/shard_map/all_to_all | solution.py:169
  348.4 4.8 all-to-all-start
  353.2 5.5 fusion.1
  358.7 1.3 slice_bitcast_fusion
  360.0 1.5 collective-permute-start.4
  361.8 20.8 %collective-permute-done.5.refs_3_ = bf16[2,2,32,8,512]{4,3,2,1,0:T(8,128)(2,1)S(1)} collective-permute-done((bf16[2,2,32,8,512]{4,3,2,1,0:T(8,128)(2,1)S(1)}, bf16[2,2,32,8,512]{4,3,2,1,0:T(8,128)(2,1)S(1)}, u32[]{:S(2)}, u32[]{:S(2)}) %collective-permute-start.5) | collective-permute-done | bytes 1048608 | tf_op jit(solution)/shard_map/ppermute | solution.py:165
  382.6 25.3 %collective-permute-done.4.refs_2_ = bf16[2,2,32,8,512]{4,3,2,1,0:T(8,128)(2,1)S(1)} collective-permute-done((bf16[2,2,32,8,512]{4,3,2,1,0:T(8,128)(2,1)S(1)}, bf16[2,2,32,8,512]{4,3,2,1,0:T(8,128)(2,1)S(1)}, u32[]{:S(2)}, u32[]{:S(2)}) %collective-permute-start.4) | collective-permute-done | bytes 1048608 | tf_op jit(solution)/shard_map/ppermute | solution.py:165
  409.2 34.8 %shard_map.74 = bf16[8,32,96,128]{3,2,1,0:T(8,128)(2,1)} custom-call(bf16[2,2,32,8,512]{4,3,2,1,0:T(8,128)(2,1)} %get-tuple-element.12.refs_0_, bf16[2,2,32,8,512]{4,3,2,1,0:T(8,128)(2,1)} %copy-done.4, bf16[2,2,32,8,512]{4,3,2,1,0:T(8,128)(2,1)} %copy-done.2, bf16[2,2,32,8,512]{4,3,2,1,0:T(8,128)(2,1)} %copy-done, bf16[64,512,768]{2,1,0:T(8,128)(2,1)} %refs_4_.10, ...), custom_call_target="tpu_custom_call" | custom-call | flops 8053063680 | bytes 31457280 | tf_op jit(solution)/shard_map/pallas_call | solution.py:46
  444.0 46.3 %all-to-all-done = bf16[8,32,96,128]{3,2,1,0:T(8,128)(2,1)} async-done(((bf16[8,32,96,128]{3,2,1,0:T(8,128)(2,1)}), bf16[8,32,96,128]{3,2,1,0:T(8,128)(2,1)}, u32[]{:S(2)}, u32[]{:S(2)}) %all-to-all-start) | async-done | bytes 6291488 | tf_op jit(solution)/shard_map/all_to_all | solution.py:169
  490.3 5.0 all-to-all-start.1
  495.5 13.7 %multiply_convert_fusion.5 = (bf16[1,8,64,1536]{3,2,1,0:T(8,128)(2,1)S(1)}, bf16[1,8,64,1536]{3,2,1,0:T(8,128)(2,1)S(1)}) fusion(f32[8,64]{1,0:T(8,128)S(1)} %mul.148, s32[8,64]{1,0:T(8,128)S(1)} %mul.142, f32[8,64]{1,0:T(8,128)S(1)} %mul.140), kind=kLoop, calls=%fused_computation.31 | loop fusion | flops 10223616 | bytes 3151872 | tf_op jit(solution)/shard_map/convert.1
  509.9 1.9 pad_maximum_fusion.refs_2_
  511.9 1.9 pad_maximum_fusion.1.refs_3_
  513.8 2.8 copy.13
  516.6 6.2 copy.17
  522.8 6.3 copy.15
  529.8 38.9 %shard_map.78.refs_4_ = f32[96,8,1536]{2,1,0:T(8,128)} custom-call(bf16[96,128,128]{2,1,0:T(8,128)(2,1)} %bitcast.120, bf16[96,192,128]{2,1,0:T(8,128)(2,1)} %bitcast.117, bf16[96,192,128]{2,1,0:T(8,128)(2,1)} %bitcast.116, bf16[1024,1536]{1,0:T(8,128)(2,1)} %pad_maximum_fusion.1.refs_3_, bf16[96,16,8,1536]{3,2,1,0:T(8,128)(2,1)} %refs_3_.1, ...), custom_call_target="tpu_custom_call" | custom-call | flops 19327352832 | bytes 37748736 | tf_op jit(solution)/shard_map/pallas_call | solution.py:107
  568.6 7.9 %copy.9 = bf16[8,32,96,128]{3,1,0,2:T(8,128)(2,1)} copy(bf16[8,32,96,128]{3,2,1,0:T(8,128)(2,1)} %all-to-all-done) | data formatting | bytes 12582912 | tf_op jit(solution)/shard_map/all_to_all | solution.py:169
  576.5 56.0 %all-to-all-done.1 = bf16[8,32,96,128]{3,2,1,0:T(8,128)(2,1)} async-done(((bf16[8,32,96,128]{3,2,1,0:T(8,128)(2,1)}), bf16[8,32,96,128]{3,2,1,0:T(8,128)(2,1)}, u32[]{:S(2)}, u32[]{:S(2)}) %all-to-all-start.1) | async-done | bytes 6291488 | tf_op jit(solution)/shard_map/all_to_all | solution.py:169
  632.5 7.9 %copy.11 = bf16[8,32,96,128]{3,1,0,2:T(8,128)(2,1)} copy(bf16[8,32,96,128]{3,2,1,0:T(8,128)(2,1)} %all-to-all-done.1) | data formatting | bytes 12582912 | tf_op jit(solution)/shard_map/all_to_all | solution.py:169
  640.4 35.9 %shard_map.79 = bf16[96,8,1536]{2,1,0:T(8,128)(2,1)} custom-call(bf16[96,256,128]{2,1,0:T(8,128)(2,1)} %bitcast.112, bf16[96,256,128]{2,1,0:T(8,128)(2,1)} %bitcast.113, bf16[1024,1536]{1,0:T(8,128)(2,1)} %pad_maximum_fusion.refs_2_, bf16[96,16,8,1536]{3,2,1,0:T(8,128)(2,1)} %refs_3_.1, f32[96,8,1536]{2,1,0:T(8,128)} %shard_map.78.refs_4_), custom_call_target="tpu_custom_call" | custom-call | flops 19327352832 | bytes 37748736 | tf_op jit(solution)/shard_map/pallas_call | solution.py:107
  (70 shorter events, 16.3 us)
Async XLA Ops:
  0.0 3.1 copy-start.6
  4.8 4.1 copy-start.17
  5.8 14.6 %collective-permute-start.8 = (bf16[2,2,16,8,512]{4,3,2,1,0:T(8,128)(2,1)S(1)}, bf16[2,2,16,8,512]{4,3,2,1,0:T(8,128)(2,1)S(1)}, u32[]{:S(2)}, u32[]{:S(2)}) collective-permute-start(bf16[2,2,16,8,512]{4,3,2,1,0:T(8,128)(2,1)S(1)} %get-tuple-element.29), channel_id=1, source_target_pairs={{0,3},{1,0},{2,1},{3,2},{4,7},{5,4},{6,5},{7,6},{8,11},{9,8},{10,9... | collective-permute-start | bytes 1572872 | tf_op jit(solution)/shard_map/ppermute | solution.py:165
  8.2 24.4 %collective-permute-start.7 = (bf16[2,2,16,8,512]{4,3,2,1,0:T(8,128)(2,1)S(1)}, bf16[2,2,16,8,512]{4,3,2,1,0:T(8,128)(2,1)S(1)}, u32[]{:S(2)}, u32[]{:S(2)}) collective-permute-start(bf16[2,2,16,8,512]{4,3,2,1,0:T(8,128)(2,1)S(1)} %get-tuple-element.30), channel_id=1, source_target_pairs={{0,2},{1,3},{2,0},{3,1},{4,6},{5,7},{6,4},{7,5},{8,10},{9,11},{10,... | collective-permute-start | bytes 1572872 | tf_op jit(solution)/shard_map/ppermute | solution.py:165
  8.7 23.8 %collective-permute-start.6 = (bf16[2,2,16,8,512]{4,3,2,1,0:T(8,128)(2,1)S(1)}, bf16[2,2,16,8,512]{4,3,2,1,0:T(8,128)(2,1)S(1)}, u32[]{:S(2)}, u32[]{:S(2)}) collective-permute-start(bf16[2,2,16,8,512]{4,3,2,1,0:T(8,128)(2,1)S(1)} %get-tuple-element.31), channel_id=1, source_target_pairs={{0,1},{1,2},{2,3},{3,0},{4,5},{5,6},{6,7},{7,4},{8,9},{9,10},{10,1... | collective-permute-start | bytes 1572872 | tf_op jit(solution)/shard_map/ppermute | solution.py:165
  20.4 12.2 %copy-start.13 = (bf16[2,2,16,8,512]{4,3,2,1,0:T(8,128)(2,1)}, bf16[2,2,16,8,512]{4,3,2,1,0:T(8,128)(2,1)S(1)}, u32[]{:S(2)}) copy-start(bf16[2,2,16,8,512]{4,3,2,1,0:T(8,128)(2,1)S(1)} %collective-permute-done.8.refs_3_) | copy-start | bytes 1572868
  32.6 0.8 copy-start.14
  32.6 1.0 copy-start.15
  51.8 79.3 %all-to-all-start.2 = ((bf16[8,16,96,128]{3,2,1,0:T(8,128)(2,1)}), bf16[8,16,96,128]{3,2,1,0:T(8,128)(2,1)S(1)}, u32[]{:S(2)}, u32[]{:S(2)}) async-start(bf16[8,16,96,128]{3,2,1,0:T(8,128)(2,1)} %shard_map.75), calls=%async_computation.2 | async-start | bytes 6291456 | tf_op jit(solution)/shard_map/all_to_all | solution.py:169
  67.0 17.0 %collective-permute-start.14 = (bf16[2,2,24,8,512]{4,3,2,1,0:T(8,128)(2,1)S(1)}, bf16[2,2,24,8,512]{4,3,2,1,0:T(8,128)(2,1)S(1)}, u32[]{:S(2)}, u32[]{:S(2)}) collective-permute-start(bf16[2,2,24,8,512]{4,3,2,1,0:T(8,128)(2,1)S(1)} %get-tuple-element.19), channel_id=1, source_target_pairs={{0,3},{1,0},{2,1},{3,2},{4,7},{5,4},{6,5},{7,6},{8,11},{9,8},{10,9... | collective-permute-start | bytes 2359304 | tf_op jit(solution)/shard_map/ppermute | solution.py:165
  67.0 36.5 %collective-permute-start.13 = (bf16[2,2,24,8,512]{4,3,2,1,0:T(8,128)(2,1)S(1)}, bf16[2,2,24,8,512]{4,3,2,1,0:T(8,128)(2,1)S(1)}, u32[]{:S(2)}, u32[]{:S(2)}) collective-permute-start(bf16[2,2,24,8,512]{4,3,2,1,0:T(8,128)(2,1)S(1)} %get-tuple-element.20), channel_id=1, source_target_pairs={{0,2},{1,3},{2,0},{3,1},{4,6},{5,7},{6,4},{7,5},{8,10},{9,11},{10,... | collective-permute-start | bytes 2359304 | tf_op jit(solution)/shard_map/ppermute | solution.py:165
  68.4 35.2 %collective-permute-start.12 = (bf16[2,2,24,8,512]{4,3,2,1,0:T(8,128)(2,1)S(1)}, bf16[2,2,24,8,512]{4,3,2,1,0:T(8,128)(2,1)S(1)}, u32[]{:S(2)}, u32[]{:S(2)}) collective-permute-start(bf16[2,2,24,8,512]{4,3,2,1,0:T(8,128)(2,1)S(1)} %get-tuple-element.21), channel_id=1, source_target_pairs={{0,1},{1,2},{2,3},{3,0},{4,5},{5,6},{6,7},{7,4},{8,9},{9,10},{10,1... | collective-permute-start | bytes 2359304 | tf_op jit(solution)/shard_map/ppermute | solution.py:165
  83.9 19.7 %copy-start.7 = (bf16[2,2,24,8,512]{4,3,2,1,0:T(8,128)(2,1)}, bf16[2,2,24,8,512]{4,3,2,1,0:T(8,128)(2,1)S(1)}, u32[]{:S(2)}) copy-start(bf16[2,2,24,8,512]{4,3,2,1,0:T(8,128)(2,1)S(1)} %collective-permute-done.14.refs_3_) | copy-start | bytes 2359300
  103.5 0.9 copy-start.9
  103.6 1.0 copy-start.11
  131.2 108.8 %all-to-all-start.4 = ((bf16[8,24,96,128]{3,2,1,0:T(8,128)(2,1)}), bf16[8,24,96,128]{3,2,1,0:T(8,128)(2,1)}, u32[]{:S(2)}, u32[]{:S(2)}) async-start(bf16[8,24,96,128]{3,2,1,0:T(8,128)(2,1)} %shard_map.77), calls=%async_computation.4 | async-start | bytes 9437184 | tf_op jit(solution)/shard_map/all_to_all | solution.py:169
  142.8 17.9 %collective-permute-start.11 = (bf16[2,2,24,8,512]{4,3,2,1,0:T(8,128)(2,1)S(1)}, bf16[2,2,24,8,512]{4,3,2,1,0:T(8,128)(2,1)S(1)}, u32[]{:S(2)}, u32[]{:S(2)}) collective-permute-start(bf16[2,2,24,8,512]{4,3,2,1,0:T(8,128)(2,1)S(1)} %get-tuple-element.23), channel_id=1, source_target_pairs={{0,3},{1,0},{2,1},{3,2},{4,7},{5,4},{6,5},{7,6},{8,11},{9,8},{10,9... | collective-permute-start | bytes 2359304 | tf_op jit(solution)/shard_map/ppermute | solution.py:165
  142.8 34.7 %collective-permute-start.10 = (bf16[2,2,24,8,512]{4,3,2,1,0:T(8,128)(2,1)S(1)}, bf16[2,2,24,8,512]{4,3,2,1,0:T(8,128)(2,1)S(1)}, u32[]{:S(2)}, u32[]{:S(2)}) collective-permute-start(bf16[2,2,24,8,512]{4,3,2,1,0:T(8,128)(2,1)S(1)} %get-tuple-element.24), channel_id=1, source_target_pairs={{0,2},{1,3},{2,0},{3,1},{4,6},{5,7},{6,4},{7,5},{8,10},{9,11},{10,... | collective-permute-start | bytes 2359304 | tf_op jit(solution)/shard_map/ppermute | solution.py:165
  143.3 35.2 %collective-permute-start.9 = (bf16[2,2,24,8,512]{4,3,2,1,0:T(8,128)(2,1)S(1)}, bf16[2,2,24,8,512]{4,3,2,1,0:T(8,128)(2,1)S(1)}, u32[]{:S(2)}, u32[]{:S(2)}) collective-permute-start(bf16[2,2,24,8,512]{4,3,2,1,0:T(8,128)(2,1)S(1)} %get-tuple-element.25), channel_id=1, source_target_pairs={{0,1},{1,2},{2,3},{3,0},{4,5},{5,6},{6,7},{7,4},{8,9},{9,10},{10,1... | collective-permute-start | bytes 2359304 | tf_op jit(solution)/shard_map/ppermute | solution.py:165
  160.6 17.9 %copy-start.8 = (bf16[2,2,24,8,512]{4,3,2,1,0:T(8,128)(2,1)}, bf16[2,2,24,8,512]{4,3,2,1,0:T(8,128)(2,1)S(1)}, u32[]{:S(2)}) copy-start(bf16[2,2,24,8,512]{4,3,2,1,0:T(8,128)(2,1)S(1)} %collective-permute-done.11.refs_3_) | copy-start | bytes 2359300
  177.5 1.0 copy-start.10
  178.5 0.9 copy-start.12
  240.0 108.4 %all-to-all-start.3 = ((bf16[8,24,96,128]{3,2,1,0:T(8,128)(2,1)}), bf16[8,24,96,128]{3,2,1,0:T(8,128)(2,1)}, u32[]{:S(2)}, u32[]{:S(2)}) async-start(bf16[8,24,96,128]{3,2,1,0:T(8,128)(2,1)} %shard_map.76), calls=%async_computation.3 | async-start | bytes 9437184 | tf_op jit(solution)/shard_map/all_to_all | solution.py:169
  254.6 22.5 %collective-permute-start.2 = (bf16[2,2,32,8,512]{4,3,2,1,0:T(8,128)(2,1)S(1)}, bf16[2,2,32,8,512]{4,3,2,1,0:T(8,128)(2,1)S(1)}, u32[]{:S(2)}, u32[]{:S(2)}) collective-permute-start(bf16[2,2,32,8,512]{4,3,2,1,0:T(8,128)(2,1)S(1)} %get-tuple-element.13), channel_id=1, source_target_pairs={{0,3},{1,0},{2,1},{3,2},{4,7},{5,4},{6,5},{7,6},{8,11},{9,8},{10,9... | collective-permute-start | bytes 3145736 | tf_op jit(solution)/shard_map/ppermute | solution.py:165
  254.6 47.9 %collective-permute-start.1 = (bf16[2,2,32,8,512]{4,3,2,1,0:T(8,128)(2,1)S(1)}, bf16[2,2,32,8,512]{4,3,2,1,0:T(8,128)(2,1)S(1)}, u32[]{:S(2)}, u32[]{:S(2)}) collective-permute-start(bf16[2,2,32,8,512]{4,3,2,1,0:T(8,128)(2,1)S(1)} %get-tuple-element.14), channel_id=1, source_target_pairs={{0,2},{1,3},{2,0},{3,1},{4,6},{5,7},{6,4},{7,5},{8,10},{9,11},{10,... | collective-permute-start | bytes 3145736 | tf_op jit(solution)/shard_map/ppermute | solution.py:165
  256.1 46.5 %collective-permute-start = (bf16[2,2,32,8,512]{4,3,2,1,0:T(8,128)(2,1)S(1)}, bf16[2,2,32,8,512]{4,3,2,1,0:T(8,128)(2,1)S(1)}, u32[]{:S(2)}, u32[]{:S(2)}) collective-permute-start(bf16[2,2,32,8,512]{4,3,2,1,0:T(8,128)(2,1)S(1)} %get-tuple-element.15), channel_id=1, source_target_pairs={{0,1},{1,2},{2,3},{3,0},{4,5},{5,6},{6,7},{7,4},{8,9},{9,10},{10,1... | collective-permute-start | bytes 3145736 | tf_op jit(solution)/shard_map/ppermute | solution.py:165
  277.2 25.4 %copy-start.1 = (bf16[2,2,32,8,512]{4,3,2,1,0:T(8,128)(2,1)}, bf16[2,2,32,8,512]{4,3,2,1,0:T(8,128)(2,1)S(1)}, u32[]{:S(2)}) copy-start(bf16[2,2,32,8,512]{4,3,2,1,0:T(8,128)(2,1)S(1)} %collective-permute-done.2.refs_3_) | copy-start | bytes 3145732
  302.5 1.0 copy-start.3
  302.6 1.3 copy-start.5
  348.4 141.9 %all-to-all-start = ((bf16[8,32,96,128]{3,2,1,0:T(8,128)(2,1)}), bf16[8,32,96,128]{3,2,1,0:T(8,128)(2,1)}, u32[]{:S(2)}, u32[]{:S(2)}) async-start(bf16[8,32,96,128]{3,2,1,0:T(8,128)(2,1)} %shard_map.73), calls=%async_computation | async-start | bytes 12582912 | tf_op jit(solution)/shard_map/all_to_all | solution.py:169
  360.0 22.5 %collective-permute-start.5 = (bf16[2,2,32,8,512]{4,3,2,1,0:T(8,128)(2,1)S(1)}, bf16[2,2,32,8,512]{4,3,2,1,0:T(8,128)(2,1)S(1)}, u32[]{:S(2)}, u32[]{:S(2)}) collective-permute-start(bf16[2,2,32,8,512]{4,3,2,1,0:T(8,128)(2,1)S(1)} %get-tuple-element.9), channel_id=1, source_target_pairs={{0,3},{1,0},{2,1},{3,2},{4,7},{5,4},{6,5},{7,6},{8,11},{9,8},{10,9... | collective-permute-start | bytes 3145736 | tf_op jit(solution)/shard_map/ppermute | solution.py:165
  360.0 47.9 %collective-permute-start.4 = (bf16[2,2,32,8,512]{4,3,2,1,0:T(8,128)(2,1)S(1)}, bf16[2,2,32,8,512]{4,3,2,1,0:T(8,128)(2,1)S(1)}, u32[]{:S(2)}, u32[]{:S(2)}) collective-permute-start(bf16[2,2,32,8,512]{4,3,2,1,0:T(8,128)(2,1)S(1)} %get-tuple-element.10), channel_id=1, source_target_pairs={{0,2},{1,3},{2,0},{3,1},{4,6},{5,7},{6,4},{7,5},{8,10},{9,11},{10,... | collective-permute-start | bytes 3145736 | tf_op jit(solution)/shard_map/ppermute | solution.py:165
  361.5 46.5 %collective-permute-start.3 = (bf16[2,2,32,8,512]{4,3,2,1,0:T(8,128)(2,1)S(1)}, bf16[2,2,32,8,512]{4,3,2,1,0:T(8,128)(2,1)S(1)}, u32[]{:S(2)}, u32[]{:S(2)}) collective-permute-start(bf16[2,2,32,8,512]{4,3,2,1,0:T(8,128)(2,1)S(1)} %get-tuple-element.11), channel_id=1, source_target_pairs={{0,1},{1,2},{2,3},{3,0},{4,5},{5,6},{6,7},{7,4},{8,9},{9,10},{10,1... | collective-permute-start | bytes 3145736 | tf_op jit(solution)/shard_map/ppermute | solution.py:165
  382.6 25.4 %copy-start = (bf16[2,2,32,8,512]{4,3,2,1,0:T(8,128)(2,1)}, bf16[2,2,32,8,512]{4,3,2,1,0:T(8,128)(2,1)S(1)}, u32[]{:S(2)}) copy-start(bf16[2,2,32,8,512]{4,3,2,1,0:T(8,128)(2,1)S(1)} %collective-permute-done.5.refs_3_) | copy-start | bytes 3145732
  407.9 1.0 copy-start.2
  408.0 1.2 copy-start.4
  444.0 51.3 %copy-start.16 = (s32[512]{0:T(512)S(1)}, s32[512]{0:T(512)}, u32[]{:S(2)}) copy-start(s32[512]{0:T(512)} %param.11) | copy-start | bytes 6148
  490.3 142.1 %all-to-all-start.1 = ((bf16[8,32,96,128]{3,2,1,0:T(8,128)(2,1)}), bf16[8,32,96,128]{3,2,1,0:T(8,128)(2,1)}, u32[]{:S(2)}, u32[]{:S(2)}) async-start(bf16[8,32,96,128]{3,2,1,0:T(8,128)(2,1)} %shard_map.74), calls=%async_computation.1 | async-start | bytes 12582912 | tf_op jit(solution)/shard_map/all_to_all | solution.py:169
